TPU v7x, 256 devices: a whole 4x4x8 slice. The times are simulated.
256 devices in a mesh: tm: 32 (over y, z_lo, core), space: 8 (over z_hi, x).
Axes of the slice: x: 4, y: 4, z: 8 (z_hi: 2, z_lo: 4; z = z_hi * 4 + z_lo), core: 2. Of those that a mesh axis runs over, the one named last changes fastest.
Arguments:
- forcing: float32 [64, 128, 128, 128], P('tm', 'space'), may hold values from -24 to 24
- exponents: int32 [64], P('tm'), may hold values from 0 to 8
- mixing: float32 [64, 64], replicated, may hold values from -1 to 3, as said below
- unmixing: float32 [64, 64], replicated, may hold values from -1 to 1
Outputs:
- solution: float32 [64, 128, 128, 128], P('tm', 'space')
Inputs may be any that keep to these rules, and one draw needn't show every extreme that they name: unmixing is the inverse of mixing up to float32 rounding.
All inputs are finite; a program needn't handle non-finite values.
Results may differ from a plain program's by a relative error of at most 0.00027.
Values sent between devices are 32-bit elements; how exact they have to be, the bound alone decides.
A program may use at most 64 MiB of HBM per device.

v0:
```python
import jax
import jax.numpy as jnp
from jax import lax
from jax.sharding import PartitionSpec as P

exact_mode = lax.Precision.HIGHEST


def copy_for_each(x, axis):
    count = lax.axis_size(axis)
    return lax.all_to_all(jnp.broadcast_to(x[None], (count, *x.shape)), axis, 0, 0, tiled=True)


def joined_along(pieces, dim):
    pieces = jnp.moveaxis(pieces, 0, dim)
    lengths = pieces.shape
    return pieces.reshape(*lengths[:dim], lengths[dim] * lengths[dim + 1], *lengths[dim + 2 :])


def gathered_copies(x, axis, dim):
    pieces = copy_for_each(x, axis)
    return joined_along(pieces, dim)


def in_blocks(x, dim, count):
    before, after = (x.shape[:dim], x.shape[dim + 1 :])
    return jnp.moveaxis(x.reshape(*before, count, -1, *after), dim, 0)


def edges_of(length, count):
    unit = 8 if length >= 8 * count else 1
    return [length // unit * k // count * unit for k in range(1, count)]


def cut_exchange(x, axis, pieces, split_dim, concat_dim):
    blocks = in_blocks(x, split_dim, lax.axis_size(axis))
    widest = max(range(1, max(2, blocks.ndim - 1)), key=lambda d: blocks.shape[d])
    done = []
    for section in jnp.split(blocks, edges_of(blocks.shape[widest], pieces), axis=widest):
        if section.size:
            done.append(lax.all_to_all(section, axis, split_axis=0, concat_axis=0, tiled=True))
    return joined_along(jnp.concatenate(done, axis=widest), concat_dim)


def sine_matrix(length):
    ordinal = jnp.arange(length, dtype=jnp.float32) + 1.0
    angle_step = jnp.pi / (length + 1)
    return jnp.sqrt(2.0 / (length + 1.0)) * jnp.sin(
        angle_step * ordinal[:, None] * ordinal[None, :]
    )


def eigen_values(length):
    ordinal = jnp.arange(length, dtype=jnp.float32) + 1.0
    return 2.0 - 2.0 * jnp.cos(jnp.pi * ordinal / (length + 1))


def final_axis_product(values, matrix):
    return jnp.dot(values, matrix, precision=exact_mode)


def along_second(values, matrix):
    return jnp.einsum("tabc,ak->tkbc", values, matrix, precision=exact_mode)


def third_axis_product(values, matrix):
    return jnp.einsum("tabc,bk->takc", values, matrix, precision=exact_mode)


def body(forcing, exponents, mixing, unmixing):
    step_count = mixing.shape[0]
    length = forcing.shape[2]
    transform_matrix = sine_matrix(length)
    eigen_all = eigen_values(length)
    source = third_axis_product(final_axis_product(forcing, transform_matrix), transform_matrix)
    time_full = lax.all_to_all(source, "tm", split_axis=2, concat_axis=0, tiled=True)
    time_mixed_field = jnp.dot(
        unmixing, time_full.reshape(step_count, -1), precision=exact_mode
    ).reshape(time_full.shape)
    all_exponents = gathered_copies(exponents, "tm", 0)
    all_shifts = 2.0 ** (all_exponents.astype(jnp.float32) / 4.0)
    columns = cut_exchange(time_mixed_field, "space", 2, 3, 1)
    middle_part = columns.shape[2]
    last_part = columns.shape[3]
    middle_start = lax.axis_index("tm") * middle_part
    last_start = lax.axis_index("space") * last_part
    eigen_middle = lax.dynamic_slice_in_dim(eigen_all, middle_start, middle_part)
    eigen_tail = lax.dynamic_slice_in_dim(eigen_all, last_start, last_part)
    spectral_field = along_second(columns, transform_matrix)
    denom = (
        all_shifts[:, None, None, None]
        + eigen_all[None, :, None, None]
        + eigen_middle[None, None, :, None]
        + eigen_tail[None, None, None, :]
    )
    spectral_field = along_second(spectral_field / denom, transform_matrix)
    time_back = lax.all_to_all(spectral_field, "space", split_axis=1, concat_axis=3, tiled=True)
    result = jnp.dot(mixing, time_back.reshape(step_count, -1), precision=exact_mode).reshape(
        time_back.shape
    )
    final = lax.all_to_all(result, "tm", split_axis=0, concat_axis=2, tiled=True)
    final = third_axis_product(final_axis_product(final, transform_matrix), transform_matrix)
    return final


def solution(mesh):
    placed = (P("tm", "space", None, None), P("tm"), P(), P())
    return jax.shard_map(
        body, mesh=mesh, in_specs=placed, out_specs=P("tm", "space", None, None), check_vma=False
    )
```

profile of v0, /device:TPU:1, one launch (start us, length us, event | category | flops | bytes accessed | tf_op | source)
XLA Modules:
  0.0 331.1 jit_solution(8253000875963036677)
XLA Ops:
  0.0 0.0 copy-start
  0.0 1.6 copy-done
  1.6 2.2 fusion.19
  3.8 2.2 fusion.8
  6.0 1.2 copy.26
  7.3 0.0 copy-start.4
  7.3 60.3 %all_to_all.64 = f32[2,16,128,128]{3,1,0,2:T(8,128)S(1)} all-to-all(f32[2,16,128,128]{3,1,0,2:T(8,128)S(1)} %copy.26), channel_id=1, replica_groups=mesh['tm'=32,'space'=8] {'tm'}, dimensions={2} | all-to-all | bytes 4194304 | tf_op jit(solution)/shard_map/all_to_all | solution.py:76
  67.6 0.0 copy-done.4
  67.6 0.6 broadcast_in_dim.2
  68.2 4.5 %all-to-all-start.3 = ((s32[32,1,2]{2,1,0:T(1,128)}), s32[32,1,2]{2,1,0:T(1,128)S(1)}, u32[]{:S(2)}, u32[]{:S(2)}) async-start(s32[32,1,2]{2,1,0:T(1,128)} %broadcast_in_dim.2), calls=%async_computation.3 | async-start | bytes 32768 | tf_op jit(solution)/shard_map/all_to_all | solution.py:11
  72.7 3.1 copy.55
  75.8 0.0 copy-start.2
  75.8 3.2 reshape.92
  79.0 0.0 copy-done.2
  79.0 3.6 %convolution_bitcast_fusion.1 = f32[64,8192]{1,0:T(8,128)S(1)} fusion(f32[64,8192]{1,0:T(8,128)} %reshape.92, f32[64,64]{1,0:T(8,128)S(1)} %copy-done.2), kind=kOutput, calls=%fused_computation.1 | convolution fusion | flops 402653184 | bytes 4210688 | tf_op jit(solution)/shard_map/dot_general | solution.py:77
  82.6 2.7 copy.28
  85.4 7.2 %fusion.45 = (f32[8,32,16,4,16]{1,4,0,3,2:T(8,128)}, f32[8,32,16,4,16]{1,4,0,3,2:T(8,128)S(1)}) fusion(f32[8,64,16,4,16]{1,4,0,3,2:T(8,128)} %bitcast.72), kind=kLoop, calls=%fused_computation.56 | loop fusion | bytes 4194304 | tf_op jit(solution)/shard_map/split | solution.py:39
  92.5 2.5 copy.56
  95.0 4.8 %reshape.107 = f32[8,1,32768]{2,1,0:T(1,128)} reshape(f32[8,16,4,16,32]{4,3,2,1,0:T(8,128)} %bitcast.76) | data formatting | bytes 2097152
  99.9 0.0 all-to-all-done.3
  99.9 8.0 %all-to-all-start.2 = ((f32[8,1,32768]{2,1,0:T(1,128)}), f32[8,1,32768]{2,1,0:T(1,128)S(1)}, u32[]{:S(2)}, u32[]{:S(2)}) async-start(f32[8,1,32768]{2,1,0:T(1,128)} %reshape.107), calls=%async_computation.2 | async-start | bytes 2097152 | tf_op jit(solution)/shard_map/all_to_all | solution.py:41
  107.8 4.8 %copy.57 = f32[8,32,16,4,16]{1,4,3,2,0:T(8,128)} copy(f32[8,32,16,4,16]{1,4,0,3,2:T(8,128)} %get-tuple-element.5) | data formatting | bytes 2097152 | tf_op jit(solution)/shard_map/split | solution.py:39
  112.6 4.9 %reshape.109 = f32[8,1,32768]{2,1,0:T(1,128)} reshape(f32[8,16,4,16,32]{4,3,2,1,0:T(8,128)} %bitcast.77) | data formatting | bytes 2097152
  117.5 7.8 %all-to-all-done.2 = f32[8,1,32768]{2,1,0:T(1,128)S(1)} async-done(((f32[8,1,32768]{2,1,0:T(1,128)}), f32[8,1,32768]{2,1,0:T(1,128)S(1)}, u32[]{:S(2)}, u32[]{:S(2)}) %all-to-all-start.2) | async-done | bytes 1048608 | tf_op jit(solution)/shard_map/all_to_all | solution.py:41
  125.3 5.2 %all-to-all-start.1 = ((f32[8,1,32768]{2,1,0:T(1,128)}), f32[8,1,32768]{2,1,0:T(1,128)S(1)}, u32[]{:S(2)}, u32[]{:S(2)}) async-start(f32[8,1,32768]{2,1,0:T(1,128)} %reshape.109), calls=%async_computation.1 | async-start | bytes 2097152 | tf_op jit(solution)/shard_map/all_to_all | solution.py:41
  130.6 0.1 dynamic_slice.6
  130.6 0.1 dynamic_slice.7
  130.7 0.1 power_reduce_fusion
  130.8 0.1 pow.15
  130.9 0.1 broadcast_add_fusion.1
  131.0 0.1 broadcast_add_fusion
  131.1 0.5 broadcast.102
  131.6 3.1 reduce.4
  134.7 3.3 reshape.108
  138.0 5.5 %all-to-all-done.1 = f32[8,1,32768]{2,1,0:T(1,128)S(1)} async-done(((f32[8,1,32768]{2,1,0:T(1,128)}), f32[8,1,32768]{2,1,0:T(1,128)S(1)}, u32[]{:S(2)}, u32[]{:S(2)}) %all-to-all-start.1) | async-done | bytes 1048608 | tf_op jit(solution)/shard_map/all_to_all | solution.py:41
  143.5 3.1 reduce.5
  146.6 3.3 %reshape.110 = f32[8,16,4,16,32]{4,3,2,1,0:T(8,128)} reshape(f32[8,32768]{1,0:T(8,128)S(1)} %reduce.5) | data formatting | bytes 2097152
  150.0 4.6 %pad_maximum_fusion = f32[8,64,16,4,16]{1,4,3,2,0:T(8,128)S(1)} fusion(f32[8,32,16,4,16]{1,4,3,2,0:T(8,128)} %bitcast.73, f32[8,32,16,4,16]{1,4,3,2,0:T(8,128)} %bitcast.74), kind=kLoop, calls=%fused_computation.2 | loop fusion | flops 524288 | bytes 4194304 | tf_op jit(solution)/shard_map/concatenate | solution.py:42
  154.6 8.6 %fusion = f32[128,64,4,16]{0,1,3,2:T(8,128)S(1)} fusion(f32[64,128,4,16]{0,3,2,1:T(8,128)S(1)} %bitcast.75, f32[128]{0:T(128)S(1)} %get-tuple-element.7, f32[128]{0:T(128)S(1)} %get-tuple-element.8), kind=kOutput, calls=%fused_computation.3 | convolution fusion | flops 805339136 | bytes 4195328 | tf_op jit(solution)/shard_map/tabc,ak->tkbc/dot_general | solution.py:63
  163.2 2.1 fusion.11
  165.3 4.5 %copy.34 = f32[64,128,4,16]{0,3,2,1:T(8,128)} copy(f32[64,128,4,16]{1,0,3,2:T(8,128)S(1)} %fusion.11) | data formatting | bytes 4194304 | tf_op jit(solution)/shard_map/tabc,ak->tkbc/transpose | solution.py:63
  169.8 5.9 %reshape.111 = f32[8,1,65536]{2,1,0:T(1,128)S(1)} reshape(f32[128,4,16,64]{3,2,1,0:T(8,128)} %bitcast.78) | data formatting | bytes 4194304
  175.7 27.9 %all_to_all.65 = f32[8,1,65536]{2,1,0:T(1,128)} all-to-all(f32[8,1,65536]{2,1,0:T(1,128)S(1)} %reshape.111), channel_id=1, replica_groups=mesh['tm'=32,'space'=8] {'space'}, dimensions={0} | all-to-all | bytes 4194304 | tf_op jit(solution)/shard_map/all_to_all | solution.py:97
  203.7 7.2 %reduce.6 = f32[8,65536]{1,0:T(8,128)S(1)} reduce(f32[8,1,65536]{2,1,0:T(1,128)} %all_to_all.65, f32[]{:T(128)} %broadcast.102), dimensions={1}, to_apply=%all_to_all.51.reduce_sub_computation | reduce | bytes 4194308 | tf_op jit(solution)/shard_map/all_to_all | solution.py:97
  210.9 3.6 %reshape.112 = f32[128,4,16,64]{3,2,1,0:T(8,128)} reshape(f32[8,65536]{1,0:T(8,128)S(1)} %reduce.6) | data formatting | bytes 4194304
  214.5 0.0 copy-start.3
  214.5 2.8 copy.35
  217.3 0.0 copy-done.3
  217.3 4.8 %convolution_bitcast_fusion = f32[64,8192]{1,0:T(8,128)S(1)} fusion(f32[64,8192]{0,1:T(8,128)S(1)} %bitcast.80, f32[64,64]{1,0:T(8,128)S(1)} %copy-done.3), kind=kOutput, calls=%fused_computation | convolution fusion | flops 402653184 | bytes 4210688 | tf_op jit(solution)/shard_map/dot_general | solution.py:98
  222.1 2.4 reshape.95
  224.6 1.8 copy.36
  226.3 98.2 %all_to_all.66 = f32[64,16,4,128]{3,1,2,0:T(8,128)S(1)} all-to-all(f32[64,16,4,128]{3,1,2,0:T(8,128)S(1)} %copy.36), channel_id=1, replica_groups=mesh['tm'=32,'space'=8] {'tm'}, dimensions={0} | all-to-all | bytes 4194304 | tf_op jit(solution)/shard_map/all_to_all | solution.py:101
  324.6 0.2 copy.37
  324.8 0.0 copy-start.1
  324.8 2.6 fusion.5
  327.5 3.5 %convolution_bitcast_fusion.2 = f32[2,16,128,128]{3,2,1,0:T(8,128)} fusion(f32[2,16,128,128]{3,2,1,0:T(8,128)S(1)} %fusion.5, f32[128]{0:T(128)S(1)} %get-tuple-element.7, f32[128]{0:T(128)S(1)} %get-tuple-element.8), kind=kOutput, calls=%fused_computation.15 | convolution fusion | flops 805339136 | bytes 4195328 | tf_op jit(solution)/shard_map/tabc,bk->takc/dot_general | solution.py:67
  330.9 0.0 copy-done.1
  (2 shorter events, 0.1 us)
Async XLA Ops:
  0.0 1.6 copy-start
  7.3 60.3 %copy-start.4 = (s32[2]{0:T(128)S(1)}, s32[2]{0:T(128)}, u32[]{:S(2)}) copy-start(s32[2]{0:T(128)} %param.5) | copy-start | bytes 28
  68.2 31.7 %all-to-all-start.3 = ((s32[32,1,2]{2,1,0:T(1,128)}), s32[32,1,2]{2,1,0:T(1,128)S(1)}, u32[]{:S(2)}, u32[]{:S(2)}) async-start(s32[32,1,2]{2,1,0:T(1,128)} %broadcast_in_dim.2), calls=%async_computation.3 | async-start | bytes 32768 | tf_op jit(solution)/shard_map/all_to_all | solution.py:11
  75.8 3.2 copy-start.2
  99.9 25.4 %all-to-all-start.2 = ((f32[8,1,32768]{2,1,0:T(1,128)}), f32[8,1,32768]{2,1,0:T(1,128)S(1)}, u32[]{:S(2)}, u32[]{:S(2)}) async-start(f32[8,1,32768]{2,1,0:T(1,128)} %reshape.107), calls=%async_computation.2 | async-start | bytes 2097152 | tf_op jit(solution)/shard_map/all_to_all | solution.py:41
  125.3 18.2 %all-to-all-start.1 = ((f32[8,1,32768]{2,1,0:T(1,128)}), f32[8,1,32768]{2,1,0:T(1,128)S(1)}, u32[]{:S(2)}, u32[]{:S(2)}) async-start(f32[8,1,32768]{2,1,0:T(1,128)} %reshape.109), calls=%async_computation.1 | async-start | bytes 2097152 | tf_op jit(solution)/shard_map/all_to_all | solution.py:41
  214.5 2.8 copy-start.3
  324.8 6.1 %copy-start.1 = (f32[2,16,128,128]{3,2,1,0:T(8,128)S(1)}, f32[2,16,128,128]{3,2,1,0:T(8,128)}, u32[]{:S(2)}) copy-start(f32[2,16,128,128]{3,2,1,0:T(8,128)} %param.4) | copy-start | bytes 6291460
where the time goes:
time: 337 us; the launch traced here: 331 us
  blocking collectives  186 us (55%)
  local copies, waits for them, and re-layouts  65.3 us (19%)
  matrix products  29.6 us (9%)
  other arithmetic  18.4 us (5%)
  starting transfers between devices  17.7 us (5%)
  waiting for transfers between devices  13.3 us (4%)
    all_to_all x1, blocking collectives, body(): lax.all_to_all(result, 'tm', split_axis=0, concat_axis=2, tiled=True)  98.2 us
    all_to_all x1, blocking collectives, body(): lax.all_to_all(source, 'tm', split_axis=2, concat_axis=0, tiled=True)  60.3 us
    all_to_all x1, blocking collectives, body(): lax.all_to_all(spectral_field, 'space', split_axis=1, concat_axis=3, tile...  27.9 us
    unnamed x16, local copies, waits for them, and re-layouts  27.5 us
    split x3, local copies, waits for them, and re-layouts, cut_exchange(): jnp.split(blocks, edges_of(blocks.shape[widest], pieces), axis=widest)  14.5 us
    all_to_all x2, waiting for transfers between devices, cut_exchange(): lax.all_to_all(section, axis, split_axis=0, concat_axis=0, tiled=True)  13.3 us
    all_to_all x2, starting transfers between devices, cut_exchange(): lax.all_to_all(section, axis, split_axis=0, concat_axis=0, tiled=True)  13.2 us
    dot_general x2, matrix products, along_second(): return jnp.einsum('tabc,ak->tkbc', values, matrix, precision=exact_mode)  10.7 us
  transfers between devices with their start and end apart: 3, of which 2 were waited for; matrix products, arithmetic and copies ran while one was open for 13% of the time, Pallas kernels for 0%

commit v1 on v0

v1 whole, which is shorter than its diff:
```python
import functools

import jax
import jax.numpy as jnp
import numpy as np
from jax import lax
from jax.experimental import pallas as pl
from jax.experimental.pallas import tpu as pltpu
from jax.sharding import PartitionSpec as P

MESH = pl.DeviceIdType.MESH
F32, BF16 = jnp.float32, jnp.bfloat16
N, STEPS = 128, 64
NY, NZ, NC, NH, NX = 4, 4, 2, 2, 4
NT = NY * NZ * NC
LOCAL = N // (NH * NX)
ROWS = LOCAL * NX
HALF = N // 2
SLOTS = NT * NX


def two_parts(x):
    x = np.asarray(x, np.float32)
    high = x.astype(jnp.bfloat16)
    low = (x - high.astype(np.float32)).astype(jnp.bfloat16)
    return high, low


def constants():
    order = np.arange(1, N + 1, dtype=np.float64)
    sine = np.sqrt(2.0 / (N + 1)) * np.sin(np.pi / (N + 1) * order[:, None] * order[None, :])
    mu = 2.0 - 2.0 * np.cos(np.pi * order / (N + 1))
    both = np.zeros((2, N, 2, 2, HALF))
    for step in range(2):
        both[step, :, :, step, :] = sine.reshape(N, 2, HALF)
    both = both.reshape(2 * N, 2 * N)
    into = np.stack(two_parts(both))
    back = np.stack(two_parts(both.T))
    high, low = two_parts(sine)
    stacked = np.concatenate([high, high, low], axis=1)
    tail = np.zeros((8, N))
    for chunk in range(2):
        tail[chunk] = np.tile(mu[chunk * HALF : (chunk + 1) * HALF] + 2.0, 2)
    return into, back, stacked, tail.astype(np.float32), mu.astype(np.float32)


def split(x):
    high = x.astype(BF16)
    low = (x - high.astype(F32)).astype(BF16)
    return high, low


def dot(a, b):
    return jnp.dot(a, b, preferred_element_type=F32)


def packed_mixer(matrix):
    row = lax.broadcasted_iota(jnp.int32, (NT, STEPS), 0)
    col = lax.broadcasted_iota(jnp.int32, (NT, STEPS), 1)
    even = (col == 2 * row).astype(BF16)
    odd = (col == 2 * row + 1).astype(BF16)
    row = lax.broadcasted_iota(jnp.int32, (STEPS, STEPS), 0)
    col = lax.broadcasted_iota(jnp.int32, (STEPS, STEPS), 1)
    pos = 2 * (col - jnp.where(col >= NT, NT, 0))
    upper = jnp.where(col >= NT, 1, 0)
    even_first = (row == pos + upper).astype(BF16)
    odd_first = (row == pos + 1 - upper).astype(BF16)

    def arranged(part):
        top = dot(dot(even, part).astype(BF16), even_first)
        bottom = dot(dot(odd, part).astype(BF16), odd_first)
        return jnp.concatenate([top, bottom], axis=0).astype(BF16)

    high, low = split(matrix)
    high, low = arranged(high), arranged(low)
    return jnp.concatenate([high, high, low], axis=1)


def kernel(
    forcing, exponents, mixing, unmixing, into_c, back_c, sine_c, tail_c, mu,
    out,
    x, into, back, sine, tail, mix_v, unmix_v, mixer, unmixer,
    sent, got, work, ratio, shift, swap_out, swap_in, sent_back, got_back, half_done,
    in_sem, const_sem, send_sem, recv_sem, swap_send, swap_recv, shift_send, shift_recv,
):
    tm, space = lax.axis_index("tm"), lax.axis_index("space")
    y, z, c = tm // (NZ * NC), (tm // NC) % NZ, tm % NC
    h, sx = space // NX, space % NX
    mine = tm * NX + sx
    zs = [(z + d) % NZ for d in range(NZ)]

    def peer(dz, s):
        dx, dy, dc = s % NX, (s // NX) % NY, s // (NX * NY)
        t = ((y + dy) % NY) * (NZ * NC) + zs[dz] * NC + (c + dc) % NC
        px = (sx + dx) % NX
        return t, px

    barrier = pltpu.get_barrier_semaphore()
    for dz in range(NZ):

        @pl.loop(0 if dz else 1, NY * NX * NC)
        def _(s):
            t, px = peer(dz, s)
            pl.semaphore_signal(barrier, inc=1, device_id=(t, h * NX + px), device_id_type=MESH)

    other = (tm, (1 - h) * NX + sx)
    pl.semaphore_signal(barrier, inc=1, device_id=other, device_id_type=MESH)

    loads = [pltpu.make_async_copy(forcing, x, in_sem)]
    pairs = ((into_c, into), (back_c, back), (sine_c, sine), (tail_c, tail), (mixing, mix_v), (unmixing, unmix_v))
    loads += [pltpu.make_async_copy(a, b, const_sem.at[k]) for k, (a, b) in enumerate(pairs)]
    for load in loads:
        load.start()

    lane = lax.broadcasted_iota(jnp.int32, (8, N), 1)
    exponent = jnp.where(lane < HALF, exponents[0].astype(F32), exponents[1].astype(F32))
    my_shift = jnp.exp2(exponent * 0.25)
    shift[tm] = my_shift

    with jax.named_scope("load"):
        loads[0].wait()
        loads[1].wait()
        loads[3].wait()

    with jax.named_scope("first"):

        @pl.loop(0, LOCAL)
        def _(i):
            field = jnp.concatenate([x[0, i], x[1, i]], axis=1)
            high, low = split(field)
            field = dot(high, into[0]) + dot(low, into[0]) + dot(high, into[1])
            high, low = split(field)
            field = dot(sine[...], jnp.concatenate([high, low, high], axis=0))
            sent[0, pl.ds(i, N, stride=LOCAL), :] = field[:, :N]
            sent[1, pl.ds(i, N, stride=LOCAL), :] = field[:, N:]

    with jax.named_scope("barrier"):
        pl.semaphore_wait(barrier, SLOTS)

    def rows(slot):
        return pl.ds(pl.multiple_of(slot * LOCAL, LOCAL), LOCAL)

    def issue(stage, chunk, source, target, groups):
        for dz in groups:

            @pl.loop(0 if dz else 1, NY * NX * NC)
            def _(s):
                t, px = peer(dz, s)
                pltpu.make_async_remote_copy(
                    source.at[chunk, rows(t * NX + px)],
                    target.at[chunk, rows(mine)],
                    send_sem.at[stage, chunk],
                    recv_sem.at[stage, chunk],
                    device_id=(t, h * NX + px),
                    device_id_type=MESH,
                ).start()

    def arrived(stage, chunk, target):
        all_others = target.at[chunk, pl.ds(0, (SLOTS - 1) * LOCAL)]
        pltpu.make_async_copy(all_others, all_others, recv_sem.at[stage, chunk]).wait()

    def left(stage, chunk, source):
        all_others = source.at[chunk, pl.ds(0, (SLOTS - 1) * LOCAL)]
        pltpu.make_async_copy(all_others, all_others, send_sem.at[stage, chunk]).wait()

    def shift_copy(t, k):
        return pltpu.make_async_remote_copy(
            shift.at[tm], shift.at[tm], shift_send, shift_recv, device_id=(t, space), device_id_type=MESH
        )

    for dz in (2, 3, 1, 0):

        @pl.loop(0 if dz else 1, NY * NC)
        def _(s):
            t = ((y + s % NY) % NY) * (NZ * NC) + zs[dz] * NC + (c + s // NY) % NC
            shift_copy(t, s).start()

    with jax.named_scope("issue0"):
        issue(0, 0, sent, got, (2, 3, 1, 0))
        issue(0, 1, sent, got, (2,))
    for chunk in range(2):
        got[chunk, rows(mine), :] = sent[chunk, rows(mine), :]

    loads[4].wait()
    loads[5].wait()
    loads[6].wait()
    mixer[...] = packed_mixer(mix_v[...])
    unmixer[...] = packed_mixer(unmix_v[...])

    pltpu.make_async_copy(shift.at[pl.ds(0, NT - 1)], shift.at[pl.ds(0, NT - 1)], shift_recv).wait()
    shifts = jnp.concatenate([shift[t, 0:1, :] for t in range(NT)], axis=0)
    for chunk in range(2):
        center = shifts + mu[mine] + tail[chunk : chunk + 1, :]

        def step(s, last, chunk=chunk, center=center):
            last = 1.0 / (center - last)
            ratio[chunk, s] = last
            return last

        lax.fori_loop(0, ROWS, step, jnp.zeros((NT, N), F32), unroll=4)

    lower = lax.broadcasted_iota(jnp.int32, (NT, N), 1) < HALF

    def mixed(matrix, field):
        high, low = split(jnp.concatenate([field, pltpu.roll(field, HALF, 1)], axis=0))
        both = dot(matrix, jnp.concatenate([high, low, high], axis=0))
        return jnp.where(lower, both[:NT], both[NT:])

    def place(s):
        return s + h * (ROWS - 1 - 2 * s)

    def swap(chunk):
        return pltpu.make_async_remote_copy(
            swap_out.at[chunk], swap_in.at[chunk], swap_send.at[chunk], swap_recv.at[chunk],
            device_id=other, device_id_type=MESH,
        )

    def towards(chunk):
        with jax.named_scope("wait_got"):
            arrived(0, chunk, got)
        matrix = unmixer[...]

        def unmix(s, _):
            work[chunk, s] = mixed(matrix, got[chunk, pl.ds(place(s), NT, stride=ROWS), :])
            return _

        with jax.named_scope("unmix"):
            lax.fori_loop(0, ROWS, unmix, 0, unroll=4)

        def step(s, last):
            last = (work[chunk, s] + last) * ratio[chunk, s]
            work[chunk, s] = last
            return last

        with jax.named_scope("eliminate"):
            swap_out[chunk] = lax.fori_loop(0, ROWS, step, jnp.zeros((NT, N), F32), unroll=8)
        swap(chunk).start()

    def away(chunk):
        with jax.named_scope("wait_swap"):
            swap(chunk).wait()
        end = ratio[chunk, ROWS - 1]
        edge = (swap_out[chunk] + end * swap_in[chunk]) / (1.0 - end * end)
        work[chunk, ROWS - 1] = edge

        def step(k, last):
            s = ROWS - 2 - k
            last = work[chunk, s] + ratio[chunk, s] * last
            work[chunk, s] = last
            return last

        with jax.named_scope("back"):
            lax.fori_loop(0, ROWS - 1, step, edge, unroll=7)
        matrix = mixer[...]

        def mix(s, _):
            sent_back[chunk, pl.ds(place(s), NT, stride=ROWS), :] = mixed(matrix, work[chunk, s])
            return _

        with jax.named_scope("mix"):
            lax.fori_loop(0, ROWS, mix, 0, unroll=4)
        got_back[chunk, rows(mine), :] = sent_back[chunk, rows(mine), :]

    towards(0)
    issue(0, 1, sent, got, (3, 1, 0))
    away(0)
    issue(1, 0, sent_back, got_back, (2, 3))
    towards(1)
    issue(1, 0, sent_back, got_back, (1, 0))
    away(1)
    issue(1, 1, sent_back, got_back, (2, 3, 1, 0))

    def second(chunk, i):
        high, low = split(got_back[chunk, pl.ds(i, N, stride=LOCAL), :])
        return dot(sine[...], jnp.concatenate([high, low, high], axis=0))

    loads[2].wait()
    with jax.named_scope("wait_back0"):
        arrived(1, 0, got_back)

    with jax.named_scope("last0"):

        @pl.loop(0, LOCAL)
        def _(i):
            half_done[i] = second(0, i)

    with jax.named_scope("wait_back1"):
        arrived(1, 1, got_back)

    with jax.named_scope("last1"):

        @pl.loop(0, LOCAL)
        def _(i):
            high, low = split(jnp.concatenate([half_done[i], second(1, i)], axis=1))
            field = dot(high, back[0]) + dot(low, back[0]) + dot(high, back[1])
            out[0, i] = field[:, :N]
            out[1, i] = field[:, N:]

    for chunk in range(2):
        left(0, chunk, sent)
        left(1, chunk, sent_back)
    pltpu.make_async_copy(shift.at[pl.ds(0, NT - 1)], shift.at[pl.ds(0, NT - 1)], shift_send).wait()


def body(forcing, exponents, mixing, unmixing):
    into, back, stacked, tail, mu = constants()
    whole = pl.BlockSpec(memory_space=pltpu.HBM)
    smem = pl.BlockSpec(memory_space=pltpu.SMEM)
    dma = pltpu.SemaphoreType.DMA
    packed = (2, SLOTS * LOCAL, N)
    return pl.pallas_call(
        kernel,
        out_shape=jax.ShapeDtypeStruct(forcing.shape, F32),
        in_specs=[whole, smem, whole, whole, whole, whole, whole, whole, smem],
        out_specs=pl.BlockSpec(memory_space=pltpu.VMEM),
        scratch_shapes=[
            pltpu.VMEM(forcing.shape, F32),
            pltpu.VMEM(into.shape, BF16),
            pltpu.VMEM(back.shape, BF16),
            pltpu.VMEM(stacked.shape, BF16),
            pltpu.VMEM(tail.shape, F32),
            pltpu.VMEM((STEPS, STEPS), F32),
            pltpu.VMEM((STEPS, STEPS), F32),
            pltpu.VMEM((STEPS, 3 * STEPS), BF16),
            pltpu.VMEM((STEPS, 3 * STEPS), BF16),
            pltpu.VMEM(packed, F32),
            pltpu.VMEM(packed, F32),
            pltpu.VMEM((2, ROWS, NT, N), F32),
            pltpu.VMEM((2, ROWS, NT, N), F32),
            pltpu.VMEM((NT, 8, N), F32),
            pltpu.VMEM((2, NT, N), F32),
            pltpu.VMEM((2, NT, N), F32),
            pltpu.VMEM(packed, F32),
            pltpu.VMEM(packed, F32),
            pltpu.VMEM((LOCAL, N, N), F32),
            dma,
            dma((6,)),
            dma((2, 2)),
            dma((2, 2)),
            dma((2,)),
            dma((2,)),
            dma,
            dma,
        ],
        compiler_params=pltpu.CompilerParams(
            collective_id=0, has_side_effects=True, vmem_limit_bytes=60 * 1024 * 1024
        ),
        name="heat",
    )(forcing, exponents, mixing, unmixing, into, back, stacked, tail, mu)


def solution(mesh):
    placed = (P("tm", "space", None, None), P("tm"), P(), P())
    return jax.shard_map(
        body, mesh=mesh, in_specs=placed, out_specs=P("tm", "space", None, None), check_vma=False
    )
```

time: 337 us -> 132 us (0.39)
  the two profiles are of different devices: /device:TPU:1 before, /device:TPU:33 now
where the time goes in v1:
time: 132 us; the launch traced here: 131 us
  Pallas kernels  128 us (97%)
  local copies, waits for them, and re-layouts  3.14 us (2%)
    pallas_call x1, Pallas kernels, body(): pl.pallas_call(kernel, out_shape=jax.ShapeDtypeStruct(forcing.shape, F32)...  128 us
    unnamed x1, local copies, waits for them, and re-layouts  3.14 us

profile of v1, /device:TPU:33, one launch (start us, length us, event | category | flops | bytes accessed | tf_op | source)
XLA Modules:
  0.0 131.4 jit_solution(224321660426955640)
XLA Ops:
  0.0 128.2 %heat.1 = f32[2,16,128,128]{3,2,1,0:T(8,128)} custom-call(f32[2,16,128,128]{3,2,1,0:T(8,128)} %forcing.1, s32[2]{0:T(128)} %exponents.1, f32[64,64]{1,0:T(8,128)} %mixing.1, f32[64,64]{1,0:T(8,128)} %unmixing.1, bf16[2,256,256]{2,1,0:T(8,128)(2,1)} %constant.10.clone.into_c, bf16[2,256,256]{2,1,0:T(8,128)(2,1)} %constant.11.clone.back_c, ...), custom_call_target="tpu_custom_call" | custom-call | tf_op jit(solution)/shard_map/heat/pallas_call | solution.py:311
  128.2 3.1 %copy.11 = f32[2,16,128,128]{3,2,1,0:T(8,128)} copy(f32[2,16,128,128]{3,2,1,0:T(8,128)} %heat.1) | data formatting | bytes 4194304

commit v2 on v1

--- a/solution.py
+++ b/solution.py
@@ -34,8 +34,10 @@
     for step in range(2):
         both[step, :, :, step, :] = sine.reshape(N, 2, HALF)
     both = both.reshape(2 * N, 2 * N)
-    into = np.stack(two_parts(both))
-    back = np.stack(two_parts(both.T))
+    high, low = two_parts(both)
+    into = np.concatenate([high, high, low], axis=0)
+    high, low = two_parts(both.T)
+    back = np.concatenate([high, high, low], axis=0)
     high, low = two_parts(sine)
     stacked = np.concatenate([high, high, low], axis=1)
     tail = np.zeros((8, N))
@@ -77,10 +79,10 @@
 
 
 def kernel(
-    forcing, exponents, mixing, unmixing, into_c, back_c, sine_c, tail_c, mu,
+    forcing, exponents_c, mixing, unmixing, into_c, back_c, sine_c, tail_c, mu_c,
     out,
-    x, into, back, sine, tail, mix_v, unmix_v, mixer, unmixer,
-    sent, got, work, ratio, shift, swap_out, swap_in, sent_back, got_back, half_done,
+    exponents, mu, x, first_rows, into, back, sine, tail, mix_v, unmix_v, mixer, unmixer,
+    sent, got, work, ratio, shift, swap_out, swap_in, sent_back, got_back, last_rows,
     in_sem, const_sem, send_sem, recv_sem, swap_send, swap_recv, shift_send, shift_recv,
 ):
     tm, space = lax.axis_index("tm"), lax.axis_index("space")
@@ -88,72 +90,102 @@
     h, sx = space // NX, space % NX
     mine = tm * NX + sx
     zs = [(z + d) % NZ for d in range(NZ)]
-
-    def peer(dz, s):
-        dx, dy, dc = s % NX, (s // NX) % NY, s // (NX * NY)
-        t = ((y + dy) % NY) * (NZ * NC) + zs[dz] * NC + (c + dc) % NC
-        px = (sx + dx) % NX
-        return t, px
+    xs = [(sx + d) % NX for d in range(NX)]
+
+    quarter = LOCAL // 4
+    fields = [
+        pltpu.make_async_copy(
+            forcing.at[:, pl.ds(b * quarter, quarter)], x.at[:, pl.ds(b * quarter, quarter)], in_sem.at[b]
+        )
+        for b in range(4)
+    ]
+    pairs = (
+        (into_c, into), (sine_c, sine), (exponents_c, exponents), (mu_c, mu), (tail_c, tail),
+        (mixing, mix_v), (unmixing, unmix_v), (back_c, back),
+    )
+    loads = [pltpu.make_async_copy(a, b, const_sem.at[k]) for k, (a, b) in enumerate(pairs)]
+    for load in (loads[0], *fields, *loads[1:]):
+        load.start()
 
     barrier = pltpu.get_barrier_semaphore()
-    for dz in range(NZ):
-
-        @pl.loop(0 if dz else 1, NY * NX * NC)
-        def _(s):
-            t, px = peer(dz, s)
-            pl.semaphore_signal(barrier, inc=1, device_id=(t, h * NX + px), device_id_type=MESH)
-
     other = (tm, (1 - h) * NX + sx)
+
+    def greet(i):
+        dy, dc = 2 * (i % 2), (i // 2) % 2
+        tc = zs[i // 4] * NC + (c + dc) % NC
+        for u in range(8):
+            t = ((y + dy + u // NX) % NY) * (NZ * NC) + tc
+            pl.semaphore_signal(barrier, inc=1, device_id=(t, h * NX + xs[u % NX]), device_id_type=MESH)
+
     pl.semaphore_signal(barrier, inc=1, device_id=other, device_id_type=MESH)
 
-    loads = [pltpu.make_async_copy(forcing, x, in_sem)]
-    pairs = ((into_c, into), (back_c, back), (sine_c, sine), (tail_c, tail), (mixing, mix_v), (unmixing, unmix_v))
-    loads += [pltpu.make_async_copy(a, b, const_sem.at[k]) for k, (a, b) in enumerate(pairs)]
-    for load in loads:
-        load.start()
-
+    with jax.named_scope("greet"):
+        for b in range(16):
+            greet(b)
+
+    with jax.named_scope("load"):
+        loads[0].wait()
+        fields[0].wait()
+
+    def into_columns(i):
+        high, low = split(jnp.concatenate([x[0, i], x[1, i]], axis=1))
+        field = dot(jnp.concatenate([high, low, high], axis=1), into[...])
+        high, low = split(field)
+        first_rows[0, i] = high
+        first_rows[1, i] = low
+
+    def into_rows(i):
+        high, low = first_rows[0, i], first_rows[1, i]
+        field = dot(sine[...], jnp.concatenate([high, low, high], axis=0))
+        sent[0, pl.ds(i, N, stride=LOCAL), :] = field[:, :N]
+        sent[1, pl.ds(i, N, stride=LOCAL), :] = field[:, N:]
+
+    with jax.named_scope("first"):
+        for i in range(LOCAL):
+            if i and i % quarter == 0:
+                fields[i // quarter].wait()
+            into_columns(i)
+    with jax.named_scope("firstb"):
+        loads[1].wait()
+        for i in range(LOCAL):
+            into_rows(i)
+
+    loads[2].wait()
+    loads[3].wait()
     lane = lax.broadcasted_iota(jnp.int32, (8, N), 1)
     exponent = jnp.where(lane < HALF, exponents[0].astype(F32), exponents[1].astype(F32))
-    my_shift = jnp.exp2(exponent * 0.25)
-    shift[tm] = my_shift
-
-    with jax.named_scope("load"):
-        loads[0].wait()
-        loads[1].wait()
-        loads[3].wait()
-
-    with jax.named_scope("first"):
-
-        @pl.loop(0, LOCAL)
-        def _(i):
-            field = jnp.concatenate([x[0, i], x[1, i]], axis=1)
-            high, low = split(field)
-            field = dot(high, into[0]) + dot(low, into[0]) + dot(high, into[1])
-            high, low = split(field)
-            field = dot(sine[...], jnp.concatenate([high, low, high], axis=0))
-            sent[0, pl.ds(i, N, stride=LOCAL), :] = field[:, :N]
-            sent[1, pl.ds(i, N, stride=LOCAL), :] = field[:, N:]
+    shift[tm] = jnp.exp2(exponent * 0.25)
 
     with jax.named_scope("barrier"):
-        pl.semaphore_wait(barrier, SLOTS)
+        pl.semaphore_wait(barrier, SLOTS + 1)
 
     def rows(slot):
         return pl.ds(pl.multiple_of(slot * LOCAL, LOCAL), LOCAL)
 
     def issue(stage, chunk, source, target, groups):
+        def start(t, px):
+            pltpu.make_async_remote_copy(
+                source.at[chunk, rows(t * NX + px)],
+                target.at[chunk, rows(mine)],
+                send_sem.at[stage, chunk],
+                recv_sem.at[stage, chunk],
+                device_id=(t, h * NX + px),
+                device_id_type=MESH,
+            ).start()
+
         for dz in groups:
-
-            @pl.loop(0 if dz else 1, NY * NX * NC)
-            def _(s):
-                t, px = peer(dz, s)
-                pltpu.make_async_remote_copy(
-                    source.at[chunk, rows(t * NX + px)],
-                    target.at[chunk, rows(mine)],
-                    send_sem.at[stage, chunk],
-                    recv_sem.at[stage, chunk],
-                    device_id=(t, h * NX + px),
-                    device_id_type=MESH,
-                ).start()
+            for dc in range(NC):
+                tc = zs[dz] * NC + (c + dc) % NC
+
+                @pl.loop(0 if dz or dc else 1, NY)
+                def _(dy, tc=tc):
+                    t = ((y + dy) % NY) * (NZ * NC) + tc
+                    for dx in range(NX):
+                        start(t, xs[dx])
+
+                if not (dz or dc):
+                    for dx in range(1, NX):
+                        start(tm, xs[dx])
 
     def arrived(stage, chunk, target):
         all_others = target.at[chunk, pl.ds(0, (SLOTS - 1) * LOCAL)]
@@ -163,27 +195,29 @@
         all_others = source.at[chunk, pl.ds(0, (SLOTS - 1) * LOCAL)]
         pltpu.make_async_copy(all_others, all_others, send_sem.at[stage, chunk]).wait()
 
-    def shift_copy(t, k):
+    def shift_copy(t):
         return pltpu.make_async_remote_copy(
             shift.at[tm], shift.at[tm], shift_send, shift_recv, device_id=(t, space), device_id_type=MESH
         )
 
-    for dz in (2, 3, 1, 0):
-
-        @pl.loop(0 if dz else 1, NY * NC)
-        def _(s):
-            t = ((y + s % NY) % NY) * (NZ * NC) + zs[dz] * NC + (c + s // NY) % NC
-            shift_copy(t, s).start()
-
     with jax.named_scope("issue0"):
+        for dz in (2, 3, 1, 0):
+
+            @pl.loop(0 if dz else 1, NY * NC)
+            def _(s, dz=dz):
+                t = ((y + s % NY) % NY) * (NZ * NC) + zs[dz] * NC + (c + s // NY) % NC
+                shift_copy(t).start()
+
         issue(0, 0, sent, got, (2, 3, 1, 0))
         issue(0, 1, sent, got, (2,))
+
     for chunk in range(2):
         got[chunk, rows(mine), :] = sent[chunk, rows(mine), :]
 
     loads[4].wait()
     loads[5].wait()
     loads[6].wait()
+    loads[7].wait()
     mixer[...] = packed_mixer(mix_v[...])
     unmixer[...] = packed_mixer(unmix_v[...])
 
@@ -225,7 +259,7 @@
             return _
 
         with jax.named_scope("unmix"):
-            lax.fori_loop(0, ROWS, unmix, 0, unroll=4)
+            lax.fori_loop(0, ROWS, unmix, 0, unroll=8)
 
         def step(s, last):
             last = (work[chunk, s] + last) * ratio[chunk, s]
@@ -258,7 +292,7 @@
             return _
 
         with jax.named_scope("mix"):
-            lax.fori_loop(0, ROWS, mix, 0, unroll=4)
+            lax.fori_loop(0, ROWS, mix, 0, unroll=8)
         got_back[chunk, rows(mine), :] = sent_back[chunk, rows(mine), :]
 
     towards(0)
@@ -270,31 +304,28 @@
     away(1)
     issue(1, 1, sent_back, got_back, (2, 3, 1, 0))
 
-    def second(chunk, i):
+    def from_rows(chunk, i):
         high, low = split(got_back[chunk, pl.ds(i, N, stride=LOCAL), :])
-        return dot(sine[...], jnp.concatenate([high, low, high], axis=0))
-
-    loads[2].wait()
-    with jax.named_scope("wait_back0"):
-        arrived(1, 0, got_back)
-
-    with jax.named_scope("last0"):
-
-        @pl.loop(0, LOCAL)
-        def _(i):
-            half_done[i] = second(0, i)
-
-    with jax.named_scope("wait_back1"):
-        arrived(1, 1, got_back)
-
-    with jax.named_scope("last1"):
-
-        @pl.loop(0, LOCAL)
-        def _(i):
-            high, low = split(jnp.concatenate([half_done[i], second(1, i)], axis=1))
-            field = dot(high, back[0]) + dot(low, back[0]) + dot(high, back[1])
-            out[0, i] = field[:, :N]
-            out[1, i] = field[:, N:]
+        field = dot(sine[...], jnp.concatenate([high, low, high], axis=0))
+        high, low = split(field)
+        last_rows[0, i, :, pl.ds(chunk * N, N)] = high
+        last_rows[1, i, :, pl.ds(chunk * N, N)] = low
+
+    def from_columns(i):
+        high, low = last_rows[0, i], last_rows[1, i]
+        field = dot(jnp.concatenate([high, low, high], axis=1), back[...])
+        out[0, i] = field[:, :N]
+        out[1, i] = field[:, N:]
+
+    for chunk in range(2):
+        with jax.named_scope(f"wait_back{chunk}"):
+            arrived(1, chunk, got_back)
+        with jax.named_scope(f"last{chunk}"):
+            for i in range(LOCAL):
+                from_rows(chunk, i)
+    with jax.named_scope("last_columns"):
+        for i in range(LOCAL):
+            from_columns(i)
 
     for chunk in range(2):
         left(0, chunk, sent)
@@ -305,16 +336,18 @@
 def body(forcing, exponents, mixing, unmixing):
     into, back, stacked, tail, mu = constants()
     whole = pl.BlockSpec(memory_space=pltpu.HBM)
-    smem = pl.BlockSpec(memory_space=pltpu.SMEM)
     dma = pltpu.SemaphoreType.DMA
     packed = (2, SLOTS * LOCAL, N)
     return pl.pallas_call(
         kernel,
         out_shape=jax.ShapeDtypeStruct(forcing.shape, F32),
-        in_specs=[whole, smem, whole, whole, whole, whole, whole, whole, smem],
+        in_specs=[whole] * 9,
         out_specs=pl.BlockSpec(memory_space=pltpu.VMEM),
         scratch_shapes=[
+            pltpu.SMEM(exponents.shape, jnp.int32),
+            pltpu.SMEM(mu.shape, F32),
             pltpu.VMEM(forcing.shape, F32),
+            pltpu.VMEM((2, LOCAL, N, 2 * N), BF16),
             pltpu.VMEM(into.shape, BF16),
             pltpu.VMEM(back.shape, BF16),
             pltpu.VMEM(stacked.shape, BF16),
@@ -332,9 +365,9 @@
             pltpu.VMEM((2, NT, N), F32),
             pltpu.VMEM(packed, F32),
             pltpu.VMEM(packed, F32),
-            pltpu.VMEM((LOCAL, N, N), F32),
-            dma,
-            dma((6,)),
+            pltpu.VMEM((2, LOCAL, N, 2 * N), BF16),
+            dma((4,)),
+            dma((8,)),
             dma((2, 2)),
             dma((2, 2)),
             dma((2,)),

time: 132 us -> 115 us (0.87)
  Pallas kernels: 128 us -> 111 us
    pallas_call x1, Pallas kernels: 128 us -> 111 us  [body(): pl.pallas_call(kernel, out_shape=jax.ShapeDtypeStruct(forcing.shape, F32)...]
where the time goes in v2:
time: 115 us
  Pallas kernels  111 us (97%)
  local copies, waits for them, and re-layouts  3.14 us (3%)
    pallas_call x1, Pallas kernels, body(): pl.pallas_call(kernel, out_shape=jax.ShapeDtypeStruct(forcing.shape, F32)...  111 us
    unnamed x1, local copies, waits for them, and re-layouts  3.14 us

profile of v2, /device:TPU:33, one launch (start us, length us, event | category | flops | bytes accessed | tf_op | source)
XLA Modules:
  0.0 114.5 jit_solution(11395002521133453083)
XLA Ops:
  0.0 111.4 %heat.1 = f32[2,16,128,128]{3,2,1,0:T(8,128)} custom-call(f32[2,16,128,128]{3,2,1,0:T(8,128)} %forcing.1, s32[2]{0:T(128)} %exponents_c.1, f32[64,64]{1,0:T(8,128)} %mixing.1, f32[64,64]{1,0:T(8,128)} %unmixing.1, bf16[768,256]{1,0:T(8,128)(2,1)} %constant.10.clone.into_c, bf16[768,256]{1,0:T(8,128)(2,1)} %constant.11.clone.back_c, ...), custom_call_target="tpu_custom_call" | custom-call | tf_op jit(solution)/shard_map/heat/pallas_call | solution.py:341
  111.4 3.1 %copy.11 = f32[2,16,128,128]{3,2,1,0:T(8,128)} copy(f32[2,16,128,128]{3,2,1,0:T(8,128)} %heat.1) | data formatting | bytes 4194304

commit v3 on v2

--- a/solution.py
+++ b/solution.py
@@ -1,4 +1,4 @@
-import functools
+import itertools
 
 import jax
 import jax.numpy as jnp
@@ -17,6 +17,9 @@
 ROWS = LOCAL * NX
 HALF = N // 2
 SLOTS = NT * NX
+ORDER = (2, 1, 3, 0)
+EARLY, LATE = ORDER[:1], ORDER[1:]
+EARLY_BACK, LATE_BACK = ORDER[:1], ORDER[1:]
 
 
 def two_parts(x):
@@ -89,8 +92,10 @@
     y, z, c = tm // (NZ * NC), (tm // NC) % NZ, tm % NC
     h, sx = space // NX, space % NX
     mine = tm * NX + sx
-    zs = [(z + d) % NZ for d in range(NZ)]
+    zs = [z, z + 1 - 2 * (z % 2), (z + 2) % NZ, NZ - 1 - z]
     xs = [(sx + d) % NX for d in range(NX)]
+    ys = [(y + d) % NY for d in range(NY)]
+    cs = [(c + d) % NC for d in range(NC)]
 
     quarter = LOCAL // 4
     fields = [
@@ -110,18 +115,14 @@
     barrier = pltpu.get_barrier_semaphore()
     other = (tm, (1 - h) * NX + sx)
 
-    def greet(i):
-        dy, dc = 2 * (i % 2), (i // 2) % 2
-        tc = zs[i // 4] * NC + (c + dc) % NC
-        for u in range(8):
-            t = ((y + dy + u // NX) % NY) * (NZ * NC) + tc
-            pl.semaphore_signal(barrier, inc=1, device_id=(t, h * NX + xs[u % NX]), device_id_type=MESH)
-
     pl.semaphore_signal(barrier, inc=1, device_id=other, device_id_type=MESH)
 
     with jax.named_scope("greet"):
-        for b in range(16):
-            greet(b)
+        steps = itertools.product(range(NX), range(NY), range(NZ), range(NC))
+        farthest_first = sorted(steps, key=lambda d: -min(d[0], NX - d[0]) - min(d[1], NY - d[1]) - 2 * (d[2] > 0))
+        for dx, dy, dz, dc in farthest_first[:-2] + [(0, 0, 0, 1)]:
+            t = ys[dy] * (NZ * NC) + zs[dz] * NC + cs[dc]
+            pl.semaphore_signal(barrier, inc=1, device_id=(t, h * NX + xs[dx]), device_id_type=MESH)
 
     with jax.named_scope("load"):
         loads[0].wait()
@@ -134,21 +135,43 @@
         first_rows[0, i] = high
         first_rows[1, i] = low
 
-    def into_rows(i):
-        high, low = first_rows[0, i], first_rows[1, i]
+    def into_rows(chunk, i):
+        columns = pl.ds(chunk * N, N)
+        high, low = (
+            jnp.concatenate([first_rows[k, i, :, columns], first_rows[k, i + 1, :, columns]], axis=1) for k in range(2)
+        )
         field = dot(sine[...], jnp.concatenate([high, low, high], axis=0))
-        sent[0, pl.ds(i, N, stride=LOCAL), :] = field[:, :N]
-        sent[1, pl.ds(i, N, stride=LOCAL), :] = field[:, N:]
-
-    with jax.named_scope("first"):
-        for i in range(LOCAL):
-            if i and i % quarter == 0:
-                fields[i // quarter].wait()
-            into_columns(i)
-    with jax.named_scope("firstb"):
-        loads[1].wait()
-        for i in range(LOCAL):
-            into_rows(i)
+        sent[chunk, pl.ds(i, N, stride=LOCAL), :] = field[:, :N]
+        sent[chunk, pl.ds(i + 1, N, stride=LOCAL), :] = field[:, N:]
+
+    def rows(slot, part=0, parts=1):
+        length = LOCAL // parts
+        return pl.ds(pl.multiple_of(slot * LOCAL + part * length, length), length)
+
+    def issue(stage, chunk, source, target, groups, *part):
+        def start(t, px):
+            pltpu.make_async_remote_copy(
+                source.at[chunk, rows(t * NX + px, *part)],
+                target.at[chunk, rows(mine, *part)],
+                send_sem.at[stage, chunk],
+                recv_sem.at[stage, chunk],
+                device_id=(t, h * NX + px),
+                device_id_type=MESH,
+            ).start()
+
+        for dz in groups:
+            for dc in range(NC):
+                tc = zs[dz] * NC + (c + dc) % NC
+
+                @pl.loop(0 if dz or dc else 1, NY)
+                def _(dy, tc=tc):
+                    t = ((y + dy) % NY) * (NZ * NC) + tc
+                    for dx in range(NX):
+                        start(t, xs[dx])
+
+                if not (dz or dc):
+                    for dx in range(1, NX):
+                        start(tm, xs[dx])
 
     loads[2].wait()
     loads[3].wait()
@@ -156,61 +179,49 @@
     exponent = jnp.where(lane < HALF, exponents[0].astype(F32), exponents[1].astype(F32))
     shift[tm] = jnp.exp2(exponent * 0.25)
 
-    with jax.named_scope("barrier"):
-        pl.semaphore_wait(barrier, SLOTS + 1)
-
-    def rows(slot):
-        return pl.ds(pl.multiple_of(slot * LOCAL, LOCAL), LOCAL)
-
-    def issue(stage, chunk, source, target, groups):
-        def start(t, px):
-            pltpu.make_async_remote_copy(
-                source.at[chunk, rows(t * NX + px)],
-                target.at[chunk, rows(mine)],
-                send_sem.at[stage, chunk],
-                recv_sem.at[stage, chunk],
-                device_id=(t, h * NX + px),
-                device_id_type=MESH,
-            ).start()
-
-        for dz in groups:
-            for dc in range(NC):
-                tc = zs[dz] * NC + (c + dc) % NC
-
-                @pl.loop(0 if dz or dc else 1, NY)
-                def _(dy, tc=tc):
-                    t = ((y + dy) % NY) * (NZ * NC) + tc
-                    for dx in range(NX):
-                        start(t, xs[dx])
-
-                if not (dz or dc):
-                    for dx in range(1, NX):
-                        start(tm, xs[dx])
-
-    def arrived(stage, chunk, target):
-        all_others = target.at[chunk, pl.ds(0, (SLOTS - 1) * LOCAL)]
-        pltpu.make_async_copy(all_others, all_others, recv_sem.at[stage, chunk]).wait()
-
-    def left(stage, chunk, source):
-        all_others = source.at[chunk, pl.ds(0, (SLOTS - 1) * LOCAL)]
-        pltpu.make_async_copy(all_others, all_others, send_sem.at[stage, chunk]).wait()
-
     def shift_copy(t):
         return pltpu.make_async_remote_copy(
             shift.at[tm], shift.at[tm], shift_send, shift_recv, device_id=(t, space), device_id_type=MESH
         )
 
-    with jax.named_scope("issue0"):
-        for dz in (2, 3, 1, 0):
+    def issue_shifts():
+        for dz in ORDER:
 
             @pl.loop(0 if dz else 1, NY * NC)
             def _(s, dz=dz):
                 t = ((y + s % NY) % NY) * (NZ * NC) + zs[dz] * NC + (c + s // NY) % NC
                 shift_copy(t).start()
 
-        issue(0, 0, sent, got, (2, 3, 1, 0))
-        issue(0, 1, sent, got, (2,))
-
+    for half in range(2):
+        with jax.named_scope(f"first{half}"):
+            for i in range(half * LOCAL // 2, (half + 1) * LOCAL // 2):
+                if i and i % quarter == 0:
+                    fields[i // quarter].wait()
+                into_columns(i)
+            if not half:
+                loads[1].wait()
+            for i in range(half * LOCAL // 2, (half + 1) * LOCAL // 2, 2):
+                into_rows(0, i)
+        if not half:
+            with jax.named_scope("barrier"):
+                pl.semaphore_wait(barrier, SLOTS)
+            issue_shifts()
+        issue(0, 0, sent, got, ORDER[:1], half, 2)
+
+    def arrived(stage, chunk, target):
+        all_others = target.at[chunk, pl.ds(0, (SLOTS - 1) * LOCAL)]
+        pltpu.make_async_copy(all_others, all_others, recv_sem.at[stage, chunk]).wait()
+
+    def left(stage, chunk, source):
+        all_others = source.at[chunk, pl.ds(0, (SLOTS - 1) * LOCAL)]
+        pltpu.make_async_copy(all_others, all_others, send_sem.at[stage, chunk]).wait()
+
+    with jax.named_scope("issue0"):
+        issue(0, 0, sent, got, ORDER[1:])
+    with jax.named_scope("first2"):
+        for i in range(0, LOCAL, 2):
+            into_rows(1, i)
+    issue(0, 1, sent, got, EARLY)
     for chunk in range(2):
         got[chunk, rows(mine), :] = sent[chunk, rows(mine), :]
 
@@ -235,10 +246,11 @@
 
     lower = lax.broadcasted_iota(jnp.int32, (NT, N), 1) < HALF
 
-    def mixed(matrix, field):
-        high, low = split(jnp.concatenate([field, pltpu.roll(field, HALF, 1)], axis=0))
+    def mixed(matrix, first, second):
+        pair = [jnp.concatenate([field, pltpu.roll(field, HALF, 1)], axis=0) for field in (first, second)]
+        high, low = split(jnp.concatenate(pair, axis=1))
         both = dot(matrix, jnp.concatenate([high, low, high], axis=0))
-        return jnp.where(lower, both[:NT], both[NT:])
+        return [jnp.where(lower, both[:NT, k : k + N], both[NT:, k : k + N]) for k in (0, N)]
 
     def place(s):
         return s + h * (ROWS - 1 - 2 * s)
@@ -254,12 +266,15 @@
             arrived(0, chunk, got)
         matrix = unmixer[...]
 
-        def unmix(s, _):
-            work[chunk, s] = mixed(matrix, got[chunk, pl.ds(place(s), NT, stride=ROWS), :])
+        def unmix(k, _):
+            pair = (2 * k, 2 * k + 1)
+            mixes = mixed(matrix, *(got[chunk, pl.ds(place(s), NT, stride=ROWS), :] for s in pair))
+            for s, field in zip(pair, mixes):
+                work[chunk, s] = field
             return _
 
         with jax.named_scope("unmix"):
-            lax.fori_loop(0, ROWS, unmix, 0, unroll=8)
+            lax.fori_loop(0, ROWS // 2, unmix, 0, unroll=8)
 
         def step(s, last):
             last = (work[chunk, s] + last) * ratio[chunk, s]
@@ -287,29 +302,33 @@
             lax.fori_loop(0, ROWS - 1, step, edge, unroll=7)
         matrix = mixer[...]
 
-        def mix(s, _):
-            sent_back[chunk, pl.ds(place(s), NT, stride=ROWS), :] = mixed(matrix, work[chunk, s])
+        def mix(k, _):
+            pair = (2 * k, 2 * k + 1)
+            for s, field in zip(pair, mixed(matrix, *(work[chunk, s] for s in pair))):
+                sent_back[chunk, pl.ds(place(s), NT, stride=ROWS), :] = field
             return _
 
         with jax.named_scope("mix"):
-            lax.fori_loop(0, ROWS, mix, 0, unroll=8)
+            lax.fori_loop(0, ROWS // 2, mix, 0, unroll=8)
         got_back[chunk, rows(mine), :] = sent_back[chunk, rows(mine), :]
 
     towards(0)
-    issue(0, 1, sent, got, (3, 1, 0))
+    issue(0, 1, sent, got, LATE)
     away(0)
-    issue(1, 0, sent_back, got_back, (2, 3))
+    issue(1, 0, sent_back, got_back, EARLY_BACK)
     towards(1)
-    issue(1, 0, sent_back, got_back, (1, 0))
+    issue(1, 0, sent_back, got_back, LATE_BACK)
     away(1)
-    issue(1, 1, sent_back, got_back, (2, 3, 1, 0))
+    issue(1, 1, sent_back, got_back, ORDER)
 
     def from_rows(chunk, i):
-        high, low = split(got_back[chunk, pl.ds(i, N, stride=LOCAL), :])
+        pair = [got_back[chunk, pl.ds(i + k, N, stride=LOCAL), :] for k in range(2)]
+        high, low = split(jnp.concatenate(pair, axis=1))
         field = dot(sine[...], jnp.concatenate([high, low, high], axis=0))
         high, low = split(field)
-        last_rows[0, i, :, pl.ds(chunk * N, N)] = high
-        last_rows[1, i, :, pl.ds(chunk * N, N)] = low
+        for k in range(2):
+            last_rows[0, i + k, :, pl.ds(chunk * N, N)] = high[:, k * N : (k + 1) * N]
+            last_rows[1, i + k, :, pl.ds(chunk * N, N)] = low[:, k * N : (k + 1) * N]
 
     def from_columns(i):
         high, low = last_rows[0, i], last_rows[1, i]
@@ -317,14 +336,20 @@
         out[0, i] = field[:, :N]
         out[1, i] = field[:, N:]
 
-    for chunk in range(2):
-        with jax.named_scope(f"wait_back{chunk}"):
-            arrived(1, chunk, got_back)
-        with jax.named_scope(f"last{chunk}"):
-            for i in range(LOCAL):
-                from_rows(chunk, i)
-    with jax.named_scope("last_columns"):
-        for i in range(LOCAL):
+    with jax.named_scope("wait_back0"):
+        arrived(1, 0, got_back)
+    with jax.named_scope("last0"):
+        for i in range(0, LOCAL, 2):
+            from_rows(0, i)
+    with jax.named_scope("wait_back1"):
+        arrived(1, 1, got_back)
+    with jax.named_scope("last1"):
+        for i in range(0, LOCAL, 2):
+            from_rows(1, i)
+            if i >= 4:
+                from_columns(i - 4)
+                from_columns(i - 3)
+        for i in range(LOCAL - 4, LOCAL):
             from_columns(i)
 
     for chunk in range(2):
@@ -338,10 +363,11 @@
     whole = pl.BlockSpec(memory_space=pltpu.HBM)
     dma = pltpu.SemaphoreType.DMA
     packed = (2, SLOTS * LOCAL, N)
+    arrays = (forcing, exponents, mixing, unmixing, into, back, stacked, tail, mu)
     return pl.pallas_call(
         kernel,
         out_shape=jax.ShapeDtypeStruct(forcing.shape, F32),
-        in_specs=[whole] * 9,
+        in_specs=[whole] * len(arrays),
         out_specs=pl.BlockSpec(memory_space=pltpu.VMEM),
         scratch_shapes=[
             pltpu.SMEM(exponents.shape, jnp.int32),
@@ -376,10 +402,10 @@
             dma,
         ],
         compiler_params=pltpu.CompilerParams(
-            collective_id=0, has_side_effects=True, vmem_limit_bytes=60 * 1024 * 1024
+            collective_id=0, has_side_effects=True, vmem_limit_bytes=48 * 1024 * 1024
         ),
         name="heat",
-    )(forcing, exponents, mixing, unmixing, into, back, stacked, tail, mu)
+    )(*(pltpu.with_memory_space_constraint(jnp.asarray(a), pltpu.HBM) for a in arrays))
 
 
 def solution(mesh):

time: 115 us -> 109 us (0.948)
  Pallas kernels: 111 us -> 108 us
  local copies, waits for them, and re-layouts: 3.14 us -> 1.32 us
    pallas_call x1, Pallas kernels: 111 us -> 108 us  [body(): pl.pallas_call(kernel, out_shape=jax.ShapeDtypeStruct(forcing.shape, F32)...]
    unnamed x1, local copies, waits for them, and re-layouts: 3.14 us -> 1.32 us
where the time goes in v3:
time: 109 us
  Pallas kernels  108 us (99%)
  local copies, waits for them, and re-layouts  1.32 us (1%)
    pallas_call x1, Pallas kernels, body(): pl.pallas_call(kernel, out_shape=jax.ShapeDtypeStruct(forcing.shape, F32)...  108 us

profile of v3, /device:TPU:33, one launch (start us, length us, event | category | flops | bytes accessed | tf_op | source)
XLA Modules:
  0.0 109.2 jit_solution(7007506922373167149)
XLA Ops:
  0.0 107.9 %heat.1 = f32[2,16,128,128]{3,2,1,0:T(8,128)S(1)} custom-call(f32[2,16,128,128]{3,2,1,0:T(8,128)} %forcing.1, s32[2]{0:T(128)} %exponents_c.1, f32[64,64]{1,0:T(8,128)} %mixing.1, f32[64,64]{1,0:T(8,128)} %unmixing.1, bf16[768,256]{1,0:T(8,128)(2,1)} %constant.10.clone.into_c, bf16[768,256]{1,0:T(8,128)(2,1)} %constant.11.clone.back_c, ...), custom_call_target="tpu_custom_call" | custom-call | tf_op jit(solution)/shard_map/heat/pallas_call | solution.py:367
  107.9 1.3 %copy.11 = f32[2,16,128,128]{3,2,1,0:T(8,128)} copy(f32[2,16,128,128]{3,2,1,0:T(8,128)S(1)} %heat.1) | data formatting | bytes 4194304

commit v4 on v3

--- a/solution.py
+++ b/solution.py
@@ -20,6 +20,7 @@
 ORDER = (2, 1, 3, 0)
 EARLY, LATE = ORDER[:1], ORDER[1:]
 EARLY_BACK, LATE_BACK = ORDER[:1], ORDER[1:]
+LAST = ORDER
 
 
 def two_parts(x):
@@ -40,7 +41,7 @@
     high, low = two_parts(both)
     into = np.concatenate([high, high, low], axis=0)
     high, low = two_parts(both.T)
-    back = np.concatenate([high, high, low], axis=0)
+    back = np.stack([np.concatenate([a[k * N : (k + 1) * N] for a in (high, high, low)], axis=0) for k in range(2)])
     high, low = two_parts(sine)
     stacked = np.concatenate([high, high, low], axis=1)
     tail = np.zeros((8, N))
@@ -148,13 +149,13 @@
         length = LOCAL // parts
         return pl.ds(pl.multiple_of(slot * LOCAL + part * length, length), length)
 
-    def issue(stage, chunk, source, target, groups, *part):
+    def issue(stage, chunk, source, target, groups, *part, arrival=0):
         def start(t, px):
             pltpu.make_async_remote_copy(
                 source.at[chunk, rows(t * NX + px, *part)],
                 target.at[chunk, rows(mine, *part)],
                 send_sem.at[stage, chunk],
-                recv_sem.at[stage, chunk],
+                recv_sem.at[stage, chunk + arrival],
                 device_id=(t, h * NX + px),
                 device_id_type=MESH,
             ).start()
@@ -208,9 +209,9 @@
             issue_shifts()
         issue(0, 0, sent, got, ORDER[:1], half, 2)
 
-    def arrived(stage, chunk, target):
-        all_others = target.at[chunk, pl.ds(0, (SLOTS - 1) * LOCAL)]
-        pltpu.make_async_copy(all_others, all_others, recv_sem.at[stage, chunk]).wait()
+    def arrived(stage, chunk, target, part=0, parts=1):
+        all_others = target.at[chunk, pl.ds(0, (SLOTS - 1) * LOCAL // parts)]
+        pltpu.make_async_copy(all_others, all_others, recv_sem.at[stage, chunk + part]).wait()
 
     def left(stage, chunk, source):
         all_others = source.at[chunk, pl.ds(0, (SLOTS - 1) * LOCAL)]
@@ -285,7 +286,7 @@
             swap_out[chunk] = lax.fori_loop(0, ROWS, step, jnp.zeros((NT, N), F32), unroll=8)
         swap(chunk).start()
 
-    def away(chunk):
+    def away(chunk, groups):
         with jax.named_scope("wait_swap"):
             swap(chunk).wait()
         end = ratio[chunk, ROWS - 1]
@@ -302,24 +303,26 @@
             lax.fori_loop(0, ROWS - 1, step, edge, unroll=7)
         matrix = mixer[...]
 
-        def mix(k, _):
-            pair = (2 * k, 2 * k + 1)
-            for s, field in zip(pair, mixed(matrix, *(work[chunk, s] for s in pair))):
-                sent_back[chunk, pl.ds(place(s), NT, stride=ROWS), :] = field
-            return _
-
-        with jax.named_scope("mix"):
-            lax.fori_loop(0, ROWS // 2, mix, 0, unroll=8)
+        for part in range(2):
+
+            def mix(k, _, part=part):
+                i = (k // 4) * LOCAL + part * (LOCAL // 2) + 2 * (k % 4)
+                pair = (i, i + 1)
+                for i, field in zip(pair, mixed(matrix, *(work[chunk, place(i)] for i in pair))):
+                    sent_back[chunk, pl.ds(i, NT, stride=ROWS), :] = field
+                return _
+
+            with jax.named_scope("mix"):
+                lax.fori_loop(0, ROWS // 4, mix, 0, unroll=8)
+            issue(1, chunk, sent_back, got_back, groups, part, 2, arrival=part * chunk)
         got_back[chunk, rows(mine), :] = sent_back[chunk, rows(mine), :]
 
     towards(0)
     issue(0, 1, sent, got, LATE)
-    away(0)
-    issue(1, 0, sent_back, got_back, EARLY_BACK)
+    away(0, EARLY_BACK)
     towards(1)
     issue(1, 0, sent_back, got_back, LATE_BACK)
-    away(1)
-    issue(1, 1, sent_back, got_back, ORDER)
+    away(1, LAST)
 
     def from_rows(chunk, i):
         pair = [got_back[chunk, pl.ds(i + k, N, stride=LOCAL), :] for k in range(2)]
@@ -330,27 +333,33 @@
             last_rows[0, i + k, :, pl.ds(chunk * N, N)] = high[:, k * N : (k + 1) * N]
             last_rows[1, i + k, :, pl.ds(chunk * N, N)] = low[:, k * N : (k + 1) * N]
 
-    def from_columns(i):
-        high, low = last_rows[0, i], last_rows[1, i]
-        field = dot(jnp.concatenate([high, low, high], axis=1), back[...])
-        out[0, i] = field[:, :N]
-        out[1, i] = field[:, N:]
+    def from_columns(chunk, i):
+        columns = pl.ds(chunk * N, N)
+        high, low = last_rows[0, i, :, columns], last_rows[1, i, :, columns]
+        field = dot(jnp.concatenate([high, low, high], axis=1), back[chunk])
+        for k in range(2):
+            part = field[:, k * N : (k + 1) * N]
+            out[k, i] = out[k, i] + part if chunk else part
 
     with jax.named_scope("wait_back0"):
         arrived(1, 0, got_back)
     with jax.named_scope("last0"):
         for i in range(0, LOCAL, 2):
             from_rows(0, i)
-    with jax.named_scope("wait_back1"):
-        arrived(1, 1, got_back)
-    with jax.named_scope("last1"):
-        for i in range(0, LOCAL, 2):
-            from_rows(1, i)
-            if i >= 4:
-                from_columns(i - 4)
-                from_columns(i - 3)
-        for i in range(LOCAL - 4, LOCAL):
-            from_columns(i)
+        for i in range(LOCAL):
+            from_columns(0, i)
+    for part in range(2):
+        with jax.named_scope(f"wait_back1{part}"):
+            arrived(1, 1, got_back, part, 2)
+        with jax.named_scope(f"last1{part}"):
+            start, end = part * LOCAL // 2, (part + 1) * LOCAL // 2
+            for i in range(start, end, 2):
+                from_rows(1, i)
+                if i >= start + 4:
+                    from_columns(1, i - 4)
+                    from_columns(1, i - 3)
+            for i in range(end - 4, end):
+                from_columns(1, i)
 
     for chunk in range(2):
         left(0, chunk, sent)
@@ -395,7 +404,7 @@
             dma((4,)),
             dma((8,)),
             dma((2, 2)),
-            dma((2, 2)),
+            dma((2, 3)),
             dma((2,)),
             dma((2,)),
             dma,

time: 109 us -> 109 us (level)
  no operation moved by 1% of the time
where the time goes in v4:
time: 109 us
  Pallas kernels  108 us (99%)
  local copies, waits for them, and re-layouts  1.32 us (1%)
    pallas_call x1, Pallas kernels, body(): pl.pallas_call(kernel, out_shape=jax.ShapeDtypeStruct(forcing.shape, F32)...  108 us

profile of v4, /device:TPU:33, one launch (start us, length us, event | category | flops | bytes accessed | tf_op | source)
XLA Modules:
  0.0 108.9 jit_solution(8040563396723188435)
XLA Ops:
  0.0 107.6 %heat.1 = f32[2,16,128,128]{3,2,1,0:T(8,128)S(1)} custom-call(f32[2,16,128,128]{3,2,1,0:T(8,128)} %forcing.1, s32[2]{0:T(128)} %exponents_c.1, f32[64,64]{1,0:T(8,128)} %mixing.1, f32[64,64]{1,0:T(8,128)} %unmixing.1, bf16[768,256]{1,0:T(8,128)(2,1)} %constant.10.clone.into_c, bf16[2,384,256]{2,1,0:T(8,128)(2,1)} %constant.11.clone.back_c, ...), custom_call_target="tpu_custom_call" | custom-call | tf_op jit(solution)/shard_map/heat/pallas_call | solution.py:376
  107.6 1.3 %copy.11 = f32[2,16,128,128]{3,2,1,0:T(8,128)} copy(f32[2,16,128,128]{3,2,1,0:T(8,128)S(1)} %heat.1) | data formatting | bytes 4194304

commit v5 on v4

--- a/solution.py
+++ b/solution.py
@@ -176,7 +176,7 @@
 
     loads[2].wait()
     loads[3].wait()
-    lane = lax.broadcasted_iota(jnp.int32, (8, N), 1)
+    lane = lax.broadcasted_iota(jnp.int32, (1, N), 1)
     exponent = jnp.where(lane < HALF, exponents[0].astype(F32), exponents[1].astype(F32))
     shift[tm] = jnp.exp2(exponent * 0.25)
 
@@ -395,7 +395,7 @@
             pltpu.VMEM(packed, F32),
             pltpu.VMEM((2, ROWS, NT, N), F32),
             pltpu.VMEM((2, ROWS, NT, N), F32),
-            pltpu.VMEM((NT, 8, N), F32),
+            pltpu.VMEM((NT, 1, N), F32),
             pltpu.VMEM((2, NT, N), F32),
             pltpu.VMEM((2, NT, N), F32),
             pltpu.VMEM(packed, F32),

time: 109 us -> 107 us (0.982)
  Pallas kernels: 108 us -> 105 us
    pallas_call x1, Pallas kernels: 108 us -> 105 us  [body(): pl.pallas_call(kernel, out_shape=jax.ShapeDtypeStruct(forcing.shape, F32)...]
where the time goes in v5:
time: 107 us
  Pallas kernels  105 us (98%)
  local copies, waits for them, and re-layouts  1.32 us (1%)
    pallas_call x1, Pallas kernels, body(): pl.pallas_call(kernel, out_shape=jax.ShapeDtypeStruct(forcing.shape, F32)...  105 us

profile of v5, /device:TPU:33, one launch (start us, length us, event | category | flops | bytes accessed | tf_op | source)
XLA Modules:
  0.0 106.8 jit_solution(2826777832311028380)
XLA Ops:
  0.0 105.4 %heat.1 = f32[2,16,128,128]{3,2,1,0:T(8,128)S(1)} custom-call(f32[2,16,128,128]{3,2,1,0:T(8,128)} %forcing.1, s32[2]{0:T(128)} %exponents_c.1, f32[64,64]{1,0:T(8,128)} %mixing.1, f32[64,64]{1,0:T(8,128)} %unmixing.1, bf16[768,256]{1,0:T(8,128)(2,1)} %constant.10.clone.into_c, bf16[2,384,256]{2,1,0:T(8,128)(2,1)} %constant.11.clone.back_c, ...), custom_call_target="tpu_custom_call" | custom-call | tf_op jit(solution)/shard_map/heat/pallas_call | solution.py:376
  105.4 1.3 %copy.11 = f32[2,16,128,128]{3,2,1,0:T(8,128)} copy(f32[2,16,128,128]{3,2,1,0:T(8,128)S(1)} %heat.1) | data formatting | bytes 4194304

commit v6 on v5

--- a/solution.py
+++ b/solution.py
@@ -206,8 +206,9 @@
         if not half:
             with jax.named_scope("barrier"):
                 pl.semaphore_wait(barrier, SLOTS)
+        issue(0, 0, sent, got, ORDER[:1], half, 2)
+        if not half:
             issue_shifts()
-        issue(0, 0, sent, got, ORDER[:1], half, 2)
 
     def arrived(stage, chunk, target, part=0, parts=1):
         all_others = target.at[chunk, pl.ds(0, (SLOTS - 1) * LOCAL // parts)]

time: 107 us -> 107 us (level)
  no operation moved by 1% of the time
where the time goes in v6:
time: 107 us
  Pallas kernels  105 us (98%)
  local copies, waits for them, and re-layouts  1.32 us (1%)
    pallas_call x1, Pallas kernels, body(): pl.pallas_call(kernel, out_shape=jax.ShapeDtypeStruct(forcing.shape, F32)...  105 us

profile of v6, /device:TPU:33, one launch (start us, length us, event | category | flops | bytes accessed | tf_op | source)
XLA Modules:
  0.0 106.6 jit_solution(819351069711924332)
XLA Ops:
  0.0 105.3 %heat.1 = f32[2,16,128,128]{3,2,1,0:T(8,128)S(1)} custom-call(f32[2,16,128,128]{3,2,1,0:T(8,128)} %forcing.1, s32[2]{0:T(128)} %exponents_c.1, f32[64,64]{1,0:T(8,128)} %mixing.1, f32[64,64]{1,0:T(8,128)} %unmixing.1, bf16[768,256]{1,0:T(8,128)(2,1)} %constant.10.clone.into_c, bf16[2,384,256]{2,1,0:T(8,128)(2,1)} %constant.11.clone.back_c, ...), custom_call_target="tpu_custom_call" | custom-call | tf_op jit(solution)/shard_map/heat/pallas_call | solution.py:377
  105.3 1.3 %copy.11 = f32[2,16,128,128]{3,2,1,0:T(8,128)} copy(f32[2,16,128,128]{3,2,1,0:T(8,128)S(1)} %heat.1) | data formatting | bytes 4194304
